TPU v7x, 16 devices: a 4x2x1 block of a 4x4x4 slice. The times are simulated.
16 devices in a mesh: dp: 4 (over y, z, core), tp: 4 (over x).
Axes of the slice: x: 4, y: 2, z: 1, core: 2. Of those that a mesh axis runs over, the one named last changes fastest.
The devices are a block of a 4x4x4 slice.
Arguments:
- x: bfloat16 [256, 7168], P('dp'), parts along dimension 0
- k_cache: bfloat16 [256, 2048, 8, 128], P('dp', None, 'tp'), parts along dimension 0
- v_cache: bfloat16 [256, 2048, 8, 128], P('dp', None, 'tp'), parts along dimension 0
- gain_a: bfloat16 [7168], replicated
- wq: bfloat16 [7168, 7168], P(None, 'tp')
- wo: bfloat16 [7168, 7168], P('tp')
- gain_m: bfloat16 [7168], replicated
- w_gate: bfloat16 [7168, 20480], P(None, 'tp')
- w_up: bfloat16 [7168, 20480], P(None, 'tp')
- w_down: bfloat16 [20480, 7168], P('tp')
Outputs:
- output: bfloat16 [256, 7168], P('dp'), parts along dimension 0
There are 4 independent parts. A program takes and returns all parts, laid end to end along the dimension named above; an argument that names none is the same for every part.
All inputs are finite; a program needn't handle non-finite values.
Results may differ from a plain program's by a relative error of at most 0.017.
Values are sent between devices in bfloat16 or wider.
A program may use at most 1.5 GiB of HBM per device.

v0:
```python
import jax
import jax.numpy as jnp
from jax import lax
from jax.sharding import PartitionSpec as P

HEAD = 128
THETA = 10000


def normed(x, gain):
    wide = x.astype(jnp.float32)
    scale = lax.rsqrt(jnp.mean(wide * wide, -1, keepdims=True) + 1e-6)
    return (wide * scale * gain.astype(jnp.float32)).astype(jnp.bfloat16)


def turned(t, place, theta):
    half = t.shape[-1] // 2
    angle = place.astype(jnp.float32)[:, None] * theta ** (-jnp.arange(half, dtype=jnp.float32) / half)
    cos, sin = jnp.cos(angle)[:, None], jnp.sin(angle)[:, None]
    a, b = t[..., :half].astype(jnp.float32), t[..., half:].astype(jnp.float32)
    return jnp.concatenate([a * cos - b * sin, b * cos + a * sin], -1).astype(jnp.bfloat16)


def matmul(a, w):
    return jnp.dot(a, w, preferred_element_type=jnp.float32).astype(jnp.bfloat16)


def einsum(form, a, b):
    return jnp.einsum(form, a.astype(jnp.float32), b.astype(jnp.float32))


def seen_by(a, wq, k_cache, v_cache, head, theta):
    batch, cache, kv_heads = k_cache.shape[:3]
    place = jnp.full((batch,), cache - 1)
    q = turned(matmul(a, wq).reshape(batch, -1, head), place, theta).reshape(batch, kv_heads, -1, head)
    scores = einsum("bgsd,bugd->bgsu", q, k_cache) * head**-0.5
    weights = jax.nn.softmax(scores, -1).astype(jnp.bfloat16)
    return einsum("bgsu,bugd->bgsd", weights, v_cache).astype(jnp.bfloat16).reshape(batch, -1)


def hidden_of(b, w_gate, w_up):
    gate = jnp.dot(b, w_gate, preferred_element_type=jnp.float32)
    up = jnp.dot(b, w_up, preferred_element_type=jnp.float32)
    return (jax.nn.silu(gate) * up).astype(jnp.bfloat16)


def solution(mesh):
    def added(t, term):
        return (t.astype(jnp.float32) + lax.psum(term.astype(jnp.bfloat16), "tp").astype(jnp.float32)).astype(jnp.bfloat16)

    def step(x, k_cache, v_cache, gain_a, wq, wo, gain_m, w_gate, w_up, w_down):
        seen = seen_by(normed(x, gain_a), wq, k_cache, v_cache, HEAD, THETA)
        h = added(x, jnp.dot(seen, wo, preferred_element_type=jnp.float32))
        return added(h, jnp.dot(hidden_of(normed(h, gain_m), w_gate, w_up), w_down, preferred_element_type=jnp.float32))

    states, cache, columns, rows_of = P("dp", None), P("dp", None, "tp", None), P(None, "tp"), P("tp", None)
    return jax.shard_map(
        step,
        mesh=mesh,
        in_specs=(states, cache, cache, P(None), columns, rows_of, P(None), columns, columns, rows_of),
        out_specs=states,
        check_vma=False,
    )
```

profile of v0, /device:TPU:112, one launch (start us, length us, event | category | flops | bytes accessed | tf_op | source)
XLA Modules:
  0.0 280.9 jit_solution(8015605990214360195)
XLA Ops:
  6.5 0.0 all-reduce.3.cloned.1.call-start
  6.6 0.7 convert_element_type.63
  7.3 1.5 fusion.11
  8.8 13.3 %convolution_convert_fusion.2 = bf16[64,1792]{1,0:T(8,128)(2,1)S(1)} fusion(bf16[7168,1792]{1,0:T(8,128)(2,1)} %param.14, bf16[64,7168]{1,0:T(8,128)(2,1)} %param.10, f32[7168]{0:T(1024)S(1)} %convert_element_type.63, f32[64]{0:T(128)S(1)} %add_rsqrt_fusion.1), kind=kOutput, calls=%fused_computation.21 | convolution fusion | flops 1646116864 | bytes 26865920 | tf_op jit(solution)/shard_map/dot_general | solution.py:25
  22.1 0.2 reshape.39
  22.3 0.1 fusion.55
  22.4 0.2 fusion.32
  22.6 0.2 copy.21
  22.8 0.2 copy.22
  22.9 34.4 %fusion.3 = f32[64,2,7,2048]{3,2,1,0:T(8,128)} fusion(bf16[64,2048,2,128]{3,2,1,0:T(2,128)(2,1)} %param.11, bf16[64,2,7,64]{3,2,1,0:T(8,128)(2,1)S(1)} %copy.22, bf16[64,2,7,64]{3,2,1,0:T(8,128)(2,1)S(1)} %copy.21), kind=kOutput, calls=%fused_computation.3 | convolution fusion | flops 470220800 | bytes 74678272 | tf_op jit(solution)/shard_map/bgsd,bugd->bgsu/dot_general | solution.py:29
  57.4 8.3 %fusion.56 = f32[64,2,7]{2,1,0:T(2,128)S(1)} fusion(f32[64,2,7,2048]{3,2,1,0:T(8,128)} %fusion.3), kind=kOutput, calls=%fused_computation.62 | output fusion | flops 7342079 | bytes 7343616 | tf_op jit(solution)/shard_map/sub | solution.py:37
  65.6 34.2 %fusion.24 = bf16[64,2,7,128]{3,2,1,0:T(8,128)(2,1)S(1)} fusion(bf16[64,2048,2,128]{3,2,1,0:T(2,128)(2,1)} %param.12, f32[64,2,7]{2,1,0:T(2,128)S(1)} %fusion.56, f32[64,2,7,2048]{3,2,1,0:T(8,128)} %fusion.3), kind=kOutput, calls=%fused_computation.35 | convolution fusion | flops 479054720 | bytes 74681856 | tf_op jit(solution)/shard_map/bgsu,bugd->bgsd/dot_general | solution.py:29
  99.8 0.3 reshape.40
  100.1 0.0 copy-start.1
  100.1 0.0 copy-start
  100.1 13.9 %convolution_convert_fusion.1 = bf16[64,7168]{1,0:T(8,128)(2,1)} fusion(bf16[64,1792]{1,0:T(8,128)(2,1)S(1)} %reshape.40, bf16[1792,7168]{1,0:T(8,128)(2,1)} %param.15), kind=kOutput, calls=%fused_computation.8 | convolution fusion | flops 1644625920 | bytes 26836992 | tf_op jit(solution)/shard_map/dot_general | solution.py:53
  114.0 0.1 all-reduce.3.cloned.1.call-update
  114.0 0.1 all-reduce.5.cloned.1.call-start
  114.1 0.0 copy-done.1
  114.1 39.9 %all-reduce.3.cloned.1.call-done = bf16[64,7168]{1,0:T(8,128)(2,1)} async-done(((bf16[64,7168]{1,0:T(8,128)(2,1)}), bf16[64,7168]{1,0:T(8,128)(2,1)}) %all-reduce.3.cloned.1.call-update) | async-done | bytes 917520 | tf_op jit(solution)/shard_map/psum | solution.py:49
  154.0 0.0 copy-done
  154.0 1.6 fusion.15
  155.6 25.8 %fusion.44 = f32[64,5120]{1,0:T(8,128)S(1)} fusion(bf16[7168,5120]{1,0:T(8,128)(2,1)} %param.17, bf16[64,7168]{1,0:T(8,128)(2,1)S(1)} %get-tuple-element.6, f32[7168]{0:T(1024)S(1)} %convert_element_type.74, f32[64]{0:T(128)S(1)} %add_rsqrt_fusion), kind=kOutput, calls=%fused_computation.50 | convolution fusion | flops 4699455488 | bytes 75657472 | tf_op jit(solution)/shard_map/dot_general | solution.py:42
  181.5 25.9 %fusion.8.clone.4 = bf16[64,5120]{1,0:T(8,128)(2,1)S(1)} fusion(bf16[7168,5120]{1,0:T(8,128)(2,1)} %param.18, f32[64,5120]{1,0:T(8,128)S(1)} %fusion.44, bf16[64,7168]{1,0:T(8,128)(2,1)S(1)} %get-tuple-element.6, f32[7168]{0:T(1024)S(1)} %convert_element_type.74, f32[64]{0:T(128)S(1)} %add_rsqrt_fusion), kind=kOutput, calls=%fused_computation.12.clone.clone.clone.1 | convolution fusion | flops 4701421568 | bytes 76312832 | tf_op jit(solution)/shard_map/dot_general | solution.py:43
  207.4 26.4 %convolution_convert_fusion = bf16[64,7168]{1,0:T(8,128)(2,1)} fusion(bf16[5120,7168]{1,0:T(8,128)(2,1)} %param.19, bf16[64,5120]{1,0:T(8,128)(2,1)S(1)} %fusion.8.clone.4), kind=kOutput, calls=%fused_computation.7 | convolution fusion | flops 4698079232 | bytes 74973184 | tf_op jit(solution)/shard_map/dot_general | solution.py:54
  233.8 0.1 all-reduce.5.cloned.1.call-update
  233.9 37.9 %all-reduce.5.cloned.1.call-done = bf16[64,7168]{1,0:T(8,128)(2,1)} async-done(((bf16[64,7168]{1,0:T(8,128)(2,1)}), bf16[64,7168]{1,0:T(8,128)(2,1)}) %all-reduce.5.cloned.1.call-update) | async-done | bytes 917520 | tf_op jit(solution)/shard_map/psum | solution.py:49
  271.7 2.3 fusion.18
  (4 shorter events, 0.1 us)
Async XLA Ops:
  6.5 147.5 %all-reduce.3.cloned.1.call-start = ((), (), s32[]{:S(2)}) async-start(), calls=%async_computation | async-start | bytes 1835008 | tf_op jit(solution)/shard_map/psum | solution.py:49
  100.1 14.0 %copy-start.1 = (bf16[7168]{0:T(1024)(128)(2,1)S(1)}, bf16[7168]{0:T(1024)(128)(2,1)}, u32[]{:S(2)}) copy-start(bf16[7168]{0:T(1024)(128)(2,1)} %param.16) | copy-start | bytes 43012
  100.1 53.9 %copy-start = (bf16[64,7168]{1,0:T(8,128)(2,1)S(1)}, bf16[64,7168]{1,0:T(8,128)(2,1)}, u32[]{:S(2)}) copy-start(bf16[64,7168]{1,0:T(8,128)(2,1)} %param.10) | copy-start | bytes 2752516
  114.0 157.7 %all-reduce.5.cloned.1.call-start = ((), (), s32[]{:S(2)}) async-start(), calls=%async_computation.1 | async-start | bytes 1835008 | tf_op jit(solution)/shard_map/psum | solution.py:49
Sparse Core Ops, SparseCore 0:
  114.1 39.8 all-reduce.2
  234.0 37.6 all-reduce.4
where the time goes:
time: 281 us
  matrix products  174 us (62%)
  waiting for transfers between devices  77.9 us (28%)
  other arithmetic  14.6 us (5%)
  between operations  13.6 us (5%)
    psum x2, waiting for transfers between devices, added(): lax.psum(term.astype(jnp.bfloat16), 'tp').astype(jnp.float32)  77.8 us
    dot_general x2, matrix products, einsum(): return jnp.einsum(form, a.astype(jnp.float32), b.astype(jnp.float32))  68.6 us
    dot_general x1, matrix products, step(): jnp.dot(hidden_of(normed(h, gain_m), w_gate, w_up), w_down, preferred_ele...  26.4 us
    dot_general x1, matrix products, hidden_of(): up = jnp.dot(b, w_up, preferred_element_type=jnp.float32)  25.9 us
    dot_general x1, matrix products, hidden_of(): gate = jnp.dot(b, w_gate, preferred_element_type=jnp.float32)  25.8 us
    dot_general x1, matrix products, step(): h = added(x, jnp.dot(seen, wo, preferred_element_type=jnp.float32))  13.9 us
    dot_general x1, matrix products, matmul(): jnp.dot(a, w, preferred_element_type=jnp.float32).astype(jnp.bfloat16)  13.3 us
    sub x1, other arithmetic, seen_by(): weights = jax.nn.softmax(scores, -1).astype(jnp.bfloat16)  8.25 us
  transfers between devices with their start and end apart: 2, of which 2 were waited for; matrix products, arithmetic and copies ran while one was open for 0% of the time, Pallas kernels for 0%

commit v1 on v0

v1 whole, which is shorter than its diff:
```python
import functools

import jax
import jax.numpy as jnp
import numpy as np
from jax import lax
from jax.experimental import pallas as pl
from jax.experimental.pallas import tpu as pltpu
from jax.sharding import PartitionSpec as P

HEAD = 128
THETA = 10000
MESH = pl.DeviceIdType.MESH
BN = 256
PAD = 16
F32, BF16 = jnp.float32, jnp.bfloat16


def rows(at, size, step=16):
    return pl.ds(pl.multiple_of(at, step), size)


def product(a, w, depth, piece):
    total = None
    for k in range(0, depth, piece):
        term = jnp.dot(a(k, piece), w(k, piece), preferred_element_type=F32)
        total = term if total is None else total + term
    return total


def kernel(cfg, x_hbm, k_hbm, v_hbm, ga_ref, wq_hbm, wo_hbm, gm_ref, wg_hbm, wu_hbm, wd_hbm, turn_ref, y_ref,
           arena, x_ref, norm, qt, qs, os_, seen, terms, got, own, hb, hid, yb, sc,
           blk_sem, kv_sem, x_sem, rs_send, rs_recv, ag_send, ag_recv, rs2_send, rs2_recv, ag2_send, ag2_recv):
    n, batch, d, keys, heads, ff, chunks, reduce_at = (
        cfg["n"], cfg["batch"], cfg["d"], cfg["keys"], cfg["heads"], cfg["ff"], cfg["chunks"], cfg["reduce_at"])
    qw = heads * HEAD
    own_cols = d // n
    groups = own_cols // BN
    half = 7
    wo_at = half * d
    kv_slots = (half * d) // (2 * keys)
    pairs = batch // 2
    n_up = ff // BN
    me = lax.axis_index("tp")
    scale = HEAD ** -0.5

    def peer(rel):
        return {"tp": lax.rem(me + rel, n)}

    barrier = pltpu.get_barrier_semaphore()
    for rel in range(1, n):
        pl.semaphore_signal(barrier, inc=1, device_id=peer(rel), device_id_type=MESH)

    def wq_copy(i):
        return pltpu.make_async_copy(wq_hbm.at[:, rows(i * BN, BN, BN)], arena.at[rows(i * d, d), :], blk_sem.at[i])

    def wo_copy(i):
        return pltpu.make_async_copy(wo_hbm.at[:, rows(i * BN, BN, BN)], arena.at[rows(wo_at + i * qw, qw), :], blk_sem.at[half + i])

    def kv_copies(p):
        slot = lax.rem(p, kv_slots)
        base = slot * (2 * keys)
        return [
            pltpu.make_async_copy(src.at[2 * p + s], arena.at[rows(base + j * keys, keys), s * HEAD:(s + 1) * HEAD], kv_sem.at[slot, 2 * j + s])
            for j, src in enumerate((k_hbm, v_hbm)) for s in range(2)
        ]

    def region(t):
        r = lax.rem(t, 2 * half)
        return (lax.rem(r + 3, half) + half * (r // half)) * d

    def up_copy(j, which):
        src = (wg_hbm, wu_hbm)[which]
        t = 2 * j + which
        return pltpu.make_async_copy(src.at[:, rows(j * BN, BN, BN)], arena.at[rows(region(t), d), :], blk_sem.at[lax.rem(t, 2 * half)])

    def down_copy(e):
        g, q = e // n, lax.rem(e, n)
        col = lax.rem(me + q, n) * groups + g - (n - 1 - q) // (n - 1)
        t = 2 * n_up - 1 + e
        return pltpu.make_async_copy(wd_hbm.at[:, rows(col * BN, BN, BN)], arena.at[rows(region(t), ff), :], blk_sem.at[lax.rem(t, 2 * half)])

    def down_at(e):
        return region(2 * n_up - 1 + e)

    n_wq, n_wo = qw // BN, d // BN
    for i in range(n_wq):
        wq_copy(i).start()
    x_copy = pltpu.make_async_copy(x_hbm, x_ref, x_sem.at[0])
    x_copy.start()

    def columns(c):
        return rows(c * BN, BN, BN)

    def norm_scale(read):
        def add(c, total):
            wide = read(c).astype(F32)
            sq = wide * wide
            return total + sq[:, :128] + sq[:, 128:]
        total = lax.fori_loop(0, d // BN, add, jnp.zeros((batch, 128), F32))
        return lax.rsqrt(jnp.sum(total, -1, keepdims=True) / d + 1e-6)

    def norm_into(read, gain_ref):
        s = norm_scale(read)

        def put(c, _):
            norm[:, columns(c)] = (read(c).astype(F32) * s * gain_ref[:, columns(c)].astype(F32)).astype(BF16)
            return 0
        lax.fori_loop(0, d // BN, put, 0)

    x_copy.wait()
    norm_into(lambda c: x_ref[:, columns(c)], ga_ref)
    qs[...] = jnp.zeros_like(qs)

    def with_norm(at):
        return product(lambda k, m: norm[:, k:k + m], lambda k, m: arena[rows(at + k, m), :], d, d // 4)

    def query(i, _):
        wq_copy(i).wait()
        q = with_norm(i * d).astype(BF16).astype(F32)
        for s in range(BN // HEAD):
            t = q[:, s * HEAD:(s + 1) * HEAD]
            t = t * turn_ref[0:1, :] + pltpu.roll(t, HEAD // 2, 1) * turn_ref[1:2, :]
            qt[i * (BN // HEAD) + s] = t.astype(BF16).astype(F32)

        @pl.when(i >= 1)
        def _():
            for c in kv_copies(i - 1):
                c.start()

        def more(w, _):
            wo_copy(w).start()
            return 0
        lax.fori_loop(i * (n_wo // n_wq), (i + 1) * (n_wo // n_wq), more, 0)
        return 0

    lax.fori_loop(0, n_wq, query, 0)
    for h in range(heads):
        qs[pl.ds(h, batch, stride=PAD), :] = qt[h]

    row = lax.broadcasted_iota(jnp.int32, (2 * PAD, 512), 0)
    lane = lax.broadcasted_iota(jnp.int32, (2 * PAD, 512), 1)
    in_second = (lax.rem(row, PAD) >= heads // 2).astype(jnp.int32)
    bias = jnp.where(lax.rem(lane, 2) == in_second, 0.0, -jnp.inf).astype(F32)
    first = lax.broadcasted_iota(jnp.int32, (2 * PAD, HEAD), 0) < PAD
    pieces = keys // 512

    def attend(p, _):
        copies = kv_copies(p)
        for c in copies:
            c.wait()
        base = lax.rem(p, kv_slots) * (2 * keys)
        q = qs[rows(p * (2 * PAD), 2 * PAD), :]
        q = jnp.concatenate([jnp.where(first, q, 0.0), jnp.where(first, 0.0, q)], 1).astype(BF16)
        top = None
        for c in range(pieces):
            s = lax.dot_general(q, arena[rows(base + c * 512, 512), :], (((1,), (1,)), ((), ())), preferred_element_type=F32)
            s = s * scale + bias
            sc[:, c * 512:(c + 1) * 512] = s
            top = s if top is None else jnp.maximum(top, s)
        top = jnp.max(top, -1, keepdims=True)
        total = None
        for c in range(pieces):
            e = jnp.exp(sc[:, c * 512:(c + 1) * 512] - top)
            sc[:, c * 512:(c + 1) * 512] = e
            total = e if total is None else total + e
        inv = 1.0 / jnp.sum(total, -1, keepdims=True)
        o = None
        for c in range(pieces):
            w = (sc[:, c * 512:(c + 1) * 512] * inv).astype(BF16)
            t = jnp.dot(w, arena[rows(base + keys + c * 512, 512), :], preferred_element_type=F32)
            o = t if o is None else o + t
        os_[rows(p * (2 * PAD), 2 * PAD), :] = jnp.concatenate([o[:PAD, :HEAD], o[PAD:, HEAD:]], 0)

        @pl.when(p + kv_slots < pairs)
        def _():
            for c in kv_copies(p + kv_slots):
                c.start()

        for t, after in enumerate(cfg["after"]):
            @pl.when(p == after)
            def _():
                up_copy(t // 2, t % 2).start()
        return 0

    def rs_copy(c, rel):
        r0, r = chunks[c]
        return pltpu.make_async_remote_copy(
            src_ref=terms.at[rel - 1, :, r0:r0 + r, :], dst_ref=got.at[rel - 1, :, r0:r0 + r, :],
            send_sem=rs_send.at[c, rel - 1], recv_sem=rs_recv.at[c, rel - 1], device_id=peer(rel), device_id_type=MESH)

    def ag_copy(c, rel, owner):
        r0, r = chunks[c]
        return pltpu.make_async_remote_copy(
            src_ref=hb.at[owner, :, r0:r0 + r, :], dst_ref=hb.at[owner, :, r0:r0 + r, :],
            send_sem=ag_send.at[c, rel - 1], recv_sem=ag_recv.at[c, rel - 1], device_id=peer(rel), device_id_type=MESH)

    def project(c):
        r0, r = chunks[c]
        for h in range(heads):
            seen[r0:r0 + r, h * HEAD:(h + 1) * HEAD] = os_[pl.ds(r0 * PAD + h, r, stride=PAD), :].astype(BF16)
        for rel in [*range(1, n), 0]:
            def block(g, _):
                col = lax.rem(me + rel, n) * groups + g
                if c == 0:
                    wo_copy(col).wait()
                t = product(lambda k, m: seen[r0:r0 + r, k:k + m], lambda k, m: arena[rows(wo_at + col * qw + k, m), :], qw, qw)
                if rel:
                    terms[rel - 1, g, r0:r0 + r, :] = t.astype(BF16)
                else:
                    own[g, r0:r0 + r, :] = t
                return 0
            lax.fori_loop(0, groups, block, 0)
            if rel:
                rs_copy(c, rel).start()

    def reduce(c):
        r0, r = chunks[c]
        for rel in range(1, n):
            rs_copy(c, rel).wait_recv()

        def block(g, _):
            s = own[g, r0:r0 + r, :]
            for rel in range(1, n):
                s += got[rel - 1, g, r0:r0 + r, :].astype(F32)
            hb[me, g, r0:r0 + r, :] = (x_ref[r0:r0 + r, rows(me * own_cols + g * BN, BN, BN)].astype(F32) + s).astype(BF16)
            return 0
        lax.fori_loop(0, groups, block, 0)
        for rel in range(1, n):
            ag_copy(c, rel, me).start()

    for c, (r0, r) in enumerate(chunks):
        if c:
            mid = (r0 + reduce_at[c]) // 2
            lax.fori_loop(r0 // 2, mid, attend, 0)
            reduce(c - 1)
            lax.fori_loop(mid, (r0 + r) // 2, attend, 0)
        else:
            lax.fori_loop(r0 // 2, (r0 + r) // 2, attend, 0)
            pl.semaphore_wait(barrier, n - 1)
        project(c)
    for t in range(half, 2 * half):
        up_copy(t // 2, t % 2).start()
    last = len(chunks) - 1
    reduce(last)
    for c in range(len(chunks)):
        for rel in range(1, n):
            rs_copy(c, rel).wait_send()
            ag_copy(c, rel, me).wait_send()
            ag_copy(c, rel, lax.rem(me + n - rel, n)).wait_recv()

    norm_into(lambda c: hb[c // groups, lax.rem(c, groups)], gm_ref)

    def up(j, _):
        up_copy(j, 0).wait()
        gate = with_norm(region(2 * j))
        up_copy(j, 1).wait()
        value = with_norm(region(2 * j + 1))
        hid[:, columns(j)] = (jax.nn.silu(gate) * value).astype(BF16)

        @pl.when(j + half < n_up)
        def _():
            up_copy(j + half, 0).start()
            up_copy(j + half, 1).start()

        @pl.when(j + half >= n_up)
        def _():
            e = 2 * (j + half - n_up) + 1
            down_copy(e).start()
            down_copy(e + 1).start()
        return 0
    lax.fori_loop(0, n_up, up, 0)

    n_down = n * groups

    def down(e):
        down_copy(e).wait()
        at = down_at(e)
        t = product(lambda k, m: hid[:, k:k + m], lambda k, m: arena[rows(at + k, m), :], ff, ff // 4)

        @pl.when(e + 2 * half <= n_down)
        def _():
            down_copy(e + 2 * half).start()
        return t

    def rs2_copy(g, rel):
        return pltpu.make_async_remote_copy(
            src_ref=terms.at[rel - 1, g], dst_ref=got.at[rel - 1, g],
            send_sem=rs2_send.at[rel - 1, g], recv_sem=rs2_recv.at[rel - 1, g], device_id=peer(rel), device_id_type=MESH)

    def ag2_copy(g, rel, owner):
        return pltpu.make_async_remote_copy(
            src_ref=yb.at[owner, g], dst_ref=yb.at[owner, g],
            send_sem=ag2_send.at[rel - 1, g], recv_sem=ag2_recv.at[rel - 1, g], device_id=peer(rel), device_id_type=MESH)

    def finish(g):
        for rel in range(1, n):
            rs2_copy(g, rel).wait_recv()
        s = own[g]
        for rel in range(1, n):
            s += got[rel - 1, g].astype(F32)
        yb[me, g] = (hb[me, g].astype(F32) + s).astype(BF16)
        for rel in range(1, n):
            ag2_copy(g, rel, me).start()

    def group(g, _):
        @pl.when(g >= 1)
        def _():
            own[g - 1] = down(n * g)

        def other(rel, _):
            terms[rel - 1, g] = down(n * g + rel).astype(BF16)
            rs2_copy(g, rel).start()
            return 0
        lax.fori_loop(1, n, other, 0)

        @pl.when(g >= 1)
        def _():
            finish(g - 1)
        return 0

    lax.fori_loop(0, groups, group, 0)
    own[groups - 1] = down(n_down)
    finish(groups - 1)

    def leave(g, _):
        for rel in range(1, n):
            rs2_copy(g, rel).wait_send()
            ag2_copy(g, rel, me).wait_send()
            ag2_copy(g, rel, lax.rem(me + n - rel, n)).wait_recv()
        for o in range(n):
            y_ref[:, rows(o * own_cols + g * BN, BN, BN)] = yb[o, g]
        return 0
    lax.fori_loop(0, groups, leave, 0)


def solution(mesh):
    n = mesh.shape["tp"]

    def step(x, k_cache, v_cache, gain_a, wq, wo, gain_m, w_gate, w_up, w_down):
        batch, d = x.shape
        cache, kv_heads = k_cache.shape[1:3]
        keys = cache * kv_heads
        heads = wq.shape[1] // HEAD
        ff = w_gate.shape[1]
        half, groups = 7, d // n // BN
        kv_slots = half * d // (2 * keys)
        pairs = batch // 2
        after = []
        for t in range(half):
            r = (t + 3) % half
            need = [s for s in range(kv_slots) if s * 2 * keys < (r + 1) * d and (s + 1) * 2 * keys > r * d]
            after.append(max(p for p in range(pairs - kv_slots, pairs) if p % kv_slots in need))
        chunks = ((0, batch * 3 // 4), (batch * 3 // 4, batch // 4))
        cfg = dict(n=n, batch=batch, d=d, keys=keys, heads=heads, ff=ff, chunks=chunks, reduce_at=(0, batch // 8), after=after)

        i = np.arange(HEAD // 2)
        angle = (cache - 1) * THETA ** (-i / (HEAD // 2))
        cos, sin = np.cos(angle), np.sin(angle)
        turn = jnp.asarray(np.stack([np.concatenate([cos, cos]), np.concatenate([-sin, sin])]), F32)

        any_, vmem = pl.BlockSpec(memory_space=pl.ANY), pl.BlockSpec(memory_space=pltpu.VMEM)
        dma = pltpu.SemaphoreType.DMA
        nc = len(chunks)
        return pl.pallas_call(
            functools.partial(kernel, cfg),
            out_shape=jax.ShapeDtypeStruct(x.shape, x.dtype),
            in_specs=[any_, any_, any_, vmem, any_, any_, vmem, any_, any_, any_, vmem],
            out_specs=vmem,
            scratch_shapes=[
                pltpu.VMEM((2 * half * d, BN), BF16),
                pltpu.VMEM((batch, d), BF16),
                pltpu.VMEM((batch, d), BF16),
                pltpu.VMEM((heads, batch, HEAD), F32),
                pltpu.VMEM((batch * PAD, HEAD), F32),
                pltpu.VMEM((batch * PAD, HEAD), F32),
                pltpu.VMEM((batch, heads * HEAD), BF16),
                pltpu.VMEM((n - 1, groups, batch, BN), BF16),
                pltpu.VMEM((n - 1, groups, batch, BN), BF16),
                pltpu.VMEM((groups, batch, BN), F32),
                pltpu.VMEM((n, groups, batch, BN), BF16),
                pltpu.VMEM((batch, ff), BF16),
                pltpu.VMEM((n, groups, batch, BN), BF16),
                pltpu.VMEM((2 * PAD, keys), F32),
                dma((half + d // BN,)), dma((kv_slots, 4)), dma((1,)),
                dma((nc, n - 1)), dma((nc, n - 1)), dma((nc, n - 1)), dma((nc, n - 1)),
                dma((n - 1, groups)), dma((n - 1, groups)), dma((n - 1, groups)), dma((n - 1, groups)),
            ],
            compiler_params=pltpu.CompilerParams(collective_id=0, has_side_effects=True, vmem_limit_bytes=67043328),
        )(x, k_cache.reshape(batch, keys, HEAD), v_cache.reshape(batch, keys, HEAD), gain_a.reshape(1, d), wq, wo,
          gain_m.reshape(1, d), w_gate, w_up, w_down, turn)

    states, cache, columns_, rows_of = P("dp", None), P("dp", None, "tp", None), P(None, "tp"), P("tp", None)
    return jax.shard_map(
        step,
        mesh=mesh,
        in_specs=(states, cache, cache, P(None), columns_, rows_of, P(None), columns_, columns_, rows_of),
        out_specs=states,
        check_vma=False,
    )
```

time: 281 us -> 184 us (0.65)
  Pallas kernels: 0 us -> 178 us
  matrix products: 174 us -> 0 us
  waiting for transfers between devices: 77.9 us -> 0 us
  other arithmetic: 14.6 us -> 0 us
  between operations: 13.6 us -> 0.01 us
  local copies, waits for them, and re-layouts: 0.93 us -> 4.82 us
    pallas_call x0 -> x1, Pallas kernels: none -> 178 us  [step(): pl.pallas_call(functools.partial(kernel, cfg), out_shape=jax.ShapeDtypeSt...]
    dot_general x7 -> x0, matrix products: 174 us -> none  [the longest x2 68.6 us: einsum(): return jnp.einsum(form, a.astype(jnp.float32), b.astype(jnp.float32))]
    psum x2 -> x0, waiting for transfers between devices: 77.8 us -> none  [added(): lax.psum(term.astype(jnp.bfloat16), 'tp').astype(jnp.float32)]
    sub x1 -> x0, other arithmetic: 8.25 us -> none  [seen_by(): weights = jax.nn.softmax(scores, -1).astype(jnp.bfloat16)]
    reduce_sum x2 -> x0, other arithmetic: 3.06 us -> none  [normed(): scale = lax.rsqrt(jnp.mean(wide * wide, -1, keepdims=True) + 1e-06)]
    convert_element_type x3 -> x0, other arithmetic: 3.04 us -> none  [the longest x1 2.31 us: added(): (t.astype(jnp.float32) + lax.psum(term.astype(jnp.bfloat16), 'tp').astype...]
  transfers between devices with their start and end apart: 2 -> 0, of which waited for: 2 -> 0; matrix products, arithmetic and copies ran while one was open for 0% -> 0% of each run, Pallas kernels for 0% -> 0%
where the time goes in v1:
time: 184 us; the launch traced here: 183 us
  Pallas kernels  178 us (97%)
  local copies, waits for them, and re-layouts  4.82 us (3%)
    pallas_call x1, Pallas kernels, step(): pl.pallas_call(functools.partial(kernel, cfg), out_shape=jax.ShapeDtypeSt...  178 us

profile of v1, /device:TPU:112, one launch (start us, length us, event | category | flops | bytes accessed | tf_op | source)
XLA Modules:
  0.0 183.2 jit_solution(5286162455653635216)
XLA Ops:
  0.0 1.3 reshape.14.ga_ref
  1.3 1.3 reshape.15.gm_ref
  2.7 178.4 %shard_map.109 = bf16[64,7168]{1,0:T(8,128)(2,1)} custom-call(bf16[64,7168]{1,0:T(8,128)(2,1)} %x_hbm.1, bf16[64,4096,128]{2,1,0:T(8,128)(2,1)} %bitcast.k_hbm, bf16[64,4096,128]{2,1,0:T(8,128)(2,1)} %bitcast.1.v_hbm, bf16[1,7168]{1,0:T(2,128)(2,1)} %reshape.14.ga_ref, bf16[7168,1792]{1,0:T(8,128)(2,1)} %wq_hbm.1, bf16[1792,7168]{1,0:T(8,128)(2,1)} %wo_hbm.1, ...), custom_call_target="tpu_custom_call" | custom-call | tf_op jit(solution)/shard_map/pallas_call | solution.py:365
  181.1 2.2 %copy.13 = bf16[64,7168]{1,0:T(8,128)(2,1)} copy(bf16[64,7168]{1,0:T(8,128)(2,1)} %shard_map.109) | data formatting | bytes 1835008

commit v2 on v1

v2 whole, which is shorter than its diff:
```python
import functools

import jax
import jax.numpy as jnp
import numpy as np
from jax import lax
from jax.experimental import pallas as pl
from jax.experimental.pallas import tpu as pltpu
from jax.sharding import PartitionSpec as P

HEAD = 128
THETA = 10000
MESH = pl.DeviceIdType.MESH
BN = 256
PAD = 16
F32, BF16 = jnp.float32, jnp.bfloat16


def rows(at, size, step=16):
    return pl.ds(pl.multiple_of(at, step), size)


def product(a, w, depth, piece):
    total = None
    for k in range(0, depth, piece):
        term = jnp.dot(a(k, piece), w(k, piece), preferred_element_type=F32)
        total = term if total is None else total + term
    return total


def products(a, ws, depth, piece):
    totals = [None] * len(ws)
    for k in range(0, depth, piece):
        for i, w in enumerate(ws):
            term = jnp.dot(a(k, piece), w(k, piece), preferred_element_type=F32)
            totals[i] = term if totals[i] is None else totals[i] + term
    return totals


def kernel(cfg, x_hbm, k_hbm, v_hbm, ga_ref, wq_hbm, wo_hbm, gm_ref, wg_hbm, wu_hbm, wd_hbm, turn_ref, y_ref,
           arena, x_ref, norm, qt, qs, os_, seen, far_terms, far_got, side, terms, got, own, hb, hid, yb, sc_a, sc_b,
           blk_sem, kv_sem, x_sem, *link_sems):
    n, batch, d, keys, heads, ff, chunks = cfg["n"], cfg["batch"], cfg["d"], cfg["keys"], cfg["heads"], cfg["ff"], cfg["chunks"]
    qw = heads * HEAD
    own_cols = d // n
    groups = own_cols // BN
    half = 7
    wo_at = half * d
    kv_slots = (half * d) // (2 * keys)
    pairs = batch // 2
    n_up = ff // BN
    me = lax.axis_index("tp")
    scale = HEAD ** -0.5

    FAR, RIGHT, LEFT = 2, 1, n - 1
    to = (RIGHT, LEFT)

    def device(rel):
        return lax.rem(me + rel, n)

    barrier = pltpu.get_barrier_semaphore()
    for rel in range(1, n):
        pl.semaphore_signal(barrier, inc=1, device_id={"tp": device(rel)}, device_id_type=MESH)

    def link(kind, index, way, src, dst, rel=None):
        send, recv = link_sems[2 * kind], link_sems[2 * kind + 1]
        return pltpu.make_async_remote_copy(
            src_ref=src, dst_ref=dst, send_sem=send.at[way, index], recv_sem=recv.at[way, index],
            device_id={"tp": device(to[way] if rel is None else rel)}, device_id_type=MESH)

    def wq_copy(i):
        return pltpu.make_async_copy(wq_hbm.at[:, rows(i * BN, BN, BN)], arena.at[rows(i * d, d), :], blk_sem.at[i])

    def wo_copy(i):
        return pltpu.make_async_copy(wo_hbm.at[:, rows(i * BN, BN, BN)], arena.at[rows(wo_at + i * qw, qw), :], blk_sem.at[half + i])

    def kv_copies(p, kinds=(0, 1)):
        slot = lax.rem(p, kv_slots)
        base = slot * (2 * keys)
        return [
            pltpu.make_async_copy(src.at[2 * p + s], arena.at[rows(base + j * keys, keys), s * HEAD:(s + 1) * HEAD], kv_sem.at[slot, 2 * j + s])
            for j, src in enumerate((k_hbm, v_hbm)) if j in kinds for s in range(2)
        ]

    def region(t):
        r = lax.rem(t, 2 * half)
        return (lax.rem(r + 3, half) + half * (r // half)) * d

    def up_copy(j, which):
        src = (wg_hbm, wu_hbm)[which]
        t = 2 * j + which
        return pltpu.make_async_copy(src.at[:, rows(j * BN, BN, BN)], arena.at[rows(region(t), d), :], blk_sem.at[lax.rem(t, 2 * half)])

    OWN = 0
    half_terms = [(FAR, g) for g in range(groups)] + [(OWN, 0)]
    order = [half_terms[i:i + 2] for i in range(0, groups + 1, 2)]
    for g in range(groups):
        order.append([(RIGHT, g), (LEFT, g)])
        if g % 3 == 1:
            at = g // 3 * 2 + 1
            order.append([(OWN, at), (OWN, at + 1)])
    order.append([(OWN, groups - 2), (OWN, groups - 1)])
    blocks = [b for two in order for b in two]

    def down_copy(v):
        rel, group = blocks[v]
        t = 2 * n_up + v
        src = wd_hbm.at[:, rows((device(rel) * groups + group) * BN, BN, BN)]
        return pltpu.make_async_copy(src, arena.at[rows(region(t), ff), :], blk_sem.at[t % (2 * half)])

    n_wq, n_wo = qw // BN, d // BN
    for i in range(n_wq):
        wq_copy(i).start()
    x_copy = pltpu.make_async_copy(x_hbm, x_ref, x_sem.at[0])
    x_copy.start()

    def columns(c):
        return rows(c * BN, BN, BN)

    def norm_into(read, gain_ref, r0, r):
        def add(o, total):
            for g in range(groups):
                wide = read(o, g).astype(F32)
                sq = wide * wide
                total = total + (sq[:, :128] + sq[:, 128:])
            return total
        total = lax.fori_loop(0, n, add, jnp.zeros((r, 128), F32))
        s = lax.rsqrt(jnp.sum(total, -1, keepdims=True) / d + 1e-6)

        def put(o, _):
            for g in range(groups):
                at = columns(o * groups + g)
                norm[r0:r0 + r, at] = (read(o, g).astype(F32) * s * gain_ref[:, at].astype(F32)).astype(BF16)
            return 0
        lax.fori_loop(0, n, put, 0)

    x_copy.wait()
    norm_into(lambda o, g: x_ref[:, columns(o * groups + g)], ga_ref, 0, batch)
    qs[...] = jnp.zeros_like(qs)

    def with_norm(at):
        return product(lambda k, m: norm[:, k:k + m], lambda k, m: arena[rows(at + k, m), :], d, d // 4)

    def query(i, _):
        wq_copy(i).wait()
        q = with_norm(i * d).astype(BF16).astype(F32)
        for s in range(BN // HEAD):
            t = q[:, s * HEAD:(s + 1) * HEAD]
            t = t * turn_ref[0:1, :] + pltpu.roll(t, HEAD // 2, 1) * turn_ref[1:2, :]
            qt[i * (BN // HEAD) + s] = t.astype(BF16).astype(F32)

        @pl.when(i >= 1)
        def _():
            for c in kv_copies(i - 1):
                c.start()

        def more(w, _):
            wo_copy(w).start()
            return 0
        lax.fori_loop(i * (n_wo // n_wq), (i + 1) * (n_wo // n_wq), more, 0)
        return 0

    lax.fori_loop(0, n_wq, query, 0)
    for h in range(heads):
        qs[pl.ds(h, batch, stride=PAD), :] = qt[h]

    row = lax.broadcasted_iota(jnp.int32, (2 * PAD, 512), 0)
    lane = lax.broadcasted_iota(jnp.int32, (2 * PAD, 512), 1)
    in_second = (lax.rem(row, PAD) >= heads // 2).astype(jnp.int32)
    bias = jnp.where(lax.rem(lane, 2) == in_second, 0.0, -jnp.inf).astype(F32)
    first = lax.broadcasted_iota(jnp.int32, (2 * PAD, HEAD), 0) < PAD
    width = 512

    def kv_base(p):
        return lax.rem(p, kv_slots) * (2 * keys)

    def wait_keys(p):
        for c in kv_copies(p, (0,)):
            c.wait()

    def wait_values(p):
        for c in kv_copies(p, (1,)):
            c.wait()

    def score(p, sc):
        q = qs[rows(p * (2 * PAD), 2 * PAD), :]
        q = jnp.concatenate([jnp.where(first, q, 0.0), jnp.where(first, 0.0, q)], 1).astype(BF16)
        for c in range(0, keys, width):
            s = lax.dot_general(q, arena[rows(kv_base(p) + c, width), :], (((1,), (1,)), ((), ())), preferred_element_type=F32)
            sc[:, c:c + width] = s * scale + bias

    def see(p, sc):
        top = None
        for c in range(0, keys, width):
            s = sc[:, c:c + width]
            top = s if top is None else jnp.maximum(top, s)
        top = jnp.max(top, -1, keepdims=True)
        total = None
        for c in range(0, keys, width):
            e = jnp.exp(sc[:, c:c + width] - top)
            sc[:, c:c + width] = e
            total = e if total is None else total + e
        inv = 1.0 / jnp.sum(total, -1, keepdims=True)
        o = None
        for c in range(0, keys, BN):
            w = (sc[:, c:c + BN] * inv).astype(BF16)
            t = jnp.dot(w, arena[rows(kv_base(p) + keys + c, BN), :], preferred_element_type=F32)
            o = t if o is None else o + t
        os_[rows(p * (2 * PAD), 2 * PAD), :] = jnp.concatenate([o[:PAD, :HEAD], o[PAD:, HEAD:]], 0)

    def two_pairs(i, end):
        p = 2 * i
        wait_keys(p + 1)
        wait_values(p)
        wait_values(p + 1)
        if not end:
            wait_keys(p + 2)
        score(p + 1, sc_b)
        see(p, sc_a)
        if not end:
            score(p + 2, sc_a)
        see(p + 1, sc_b)

        if not end:
            @pl.when(p + 1 + kv_slots < pairs)
            def _():
                for c in kv_copies(p + kv_slots) + kv_copies(p + 1 + kv_slots):
                    c.start()

        for t, after in enumerate(cfg["after"]):
            if end:
                if after // 2 == i:
                    up_copy(t // 2, t % 2).start()
            elif after // 2 < pairs // 2 - 1:
                @pl.when(i == after // 2)
                def _():
                    up_copy(t // 2, t % 2).start()

    def attend(first_row, last_row):
        def step(i, _):
            two_pairs(i, False)
            return 0
        lo, hi = first_row // 4, last_row // 4
        lax.fori_loop(lo, min(hi, pairs // 2 - 1), step, 0)
        if hi == pairs // 2:
            two_pairs(hi - 1, True)

    half_lanes = (slice(0, BN // 2), slice(BN // 2, BN))

    def chunk_link(kind, c, way, owner=None):
        r0, r = chunks[c]
        straight = kind == 3 and c == len(chunks) - 1
        lanes = half_lanes[way] if kind == 3 and not straight else slice(0, BN)
        owner = me if owner is None else owner

        def at(ref, first=way):
            return ref.at[first, :, r0:r0 + r]
        if kind < 2:
            src, dst = ((far_terms, far_got), (terms, got))[kind]
            return link(kind, c, way, at(src), at(dst))
        states = hb.at[owner, :, r0:r0 + r, lanes]
        return link(kind, c, way, states, states, FAR if straight else None)

    def project(c):
        r0, r = chunks[c]
        for h in range(heads):
            seen[r0:r0 + r, h * HEAD:(h + 1) * HEAD] = os_[pl.ds(r0 * PAD + h, r, stride=PAD), :].astype(BF16)

        def owner(rel, put):
            if c == 0:
                for g in range(groups):
                    wo_copy(device(rel) * groups + g).wait()
            for g in range(groups):
                at = wo_at + (device(rel) * groups + g) * qw
                put(g, product(lambda k, m: seen[r0:r0 + r, k:k + m], lambda k, m: arena[rows(at + k, m), :], qw, qw))

        def put_far(g, t):
            for way in range(2):
                far_terms[way, g, r0:r0 + r, :] = t[:, half_lanes[way]].astype(BF16)

        def put_own(g, t):
            own[g, r0:r0 + r, :] = t

        owner(FAR, put_far)
        for way in range(2):
            chunk_link(0, c, way).start()
        for way in range(2):
            def put_side(g, t):
                side[way, g, r0:r0 + r, :] = t
            owner(to[way], put_side)
        owner(0, put_own)

    def relay(c):
        r0, r = chunks[c]
        for way in range(2):
            chunk_link(0, c, way).wait_recv()

            def block(g, _):
                for lanes in range(2):
                    t = side[way, g, r0:r0 + r, half_lanes[lanes]]
                    if lanes == way:
                        t = t + far_got[way, g, r0:r0 + r, :].astype(F32)
                    terms[way, g, r0:r0 + r, half_lanes[lanes]] = t.astype(BF16)
                return 0
            lax.fori_loop(0, groups, block, 0)
            chunk_link(1, c, way).start()

    def reduce(c):
        r0, r = chunks[c]
        for way in range(2):
            chunk_link(1, c, way).wait_recv()

        def block(g, _):
            s = own[g, r0:r0 + r, :]
            for way in range(2):
                s += got[way, g, r0:r0 + r, :].astype(F32)
            hb[me, g, r0:r0 + r, :] = (x_ref[r0:r0 + r, rows(me * own_cols + g * BN, BN, BN)].astype(F32) + s).astype(BF16)
            return 0
        lax.fori_loop(0, groups, block, 0)
        for way in range(2):
            chunk_link(2, c, way).start()
        if c == len(chunks) - 1:
            chunk_link(3, c, 0).start()

    def forward(c):
        for way in range(2):
            source = device(to[1 - way])
            chunk_link(2, c, way, source).wait_recv()
            chunk_link(3, c, way, source).start()

    wait_keys(0)
    score(0, sc_a)
    last = len(chunks) - 1
    for c, (r0, r) in enumerate(chunks):
        if c:
            attend(r0, r0 + cfg["relay_after"])
            relay(c - 1)
            attend(r0 + cfg["relay_after"], r0 + cfg["reduce_after"])
            reduce(c - 1)
            attend(r0 + cfg["reduce_after"], r0 + r)
        else:
            attend(r0, r0 + r)
            pl.semaphore_wait(barrier, n - 1)
        project(c)
    for t in range(half, 2 * half):
        up_copy(t // 2, t % 2).start()
    def norm_chunk(c):
        r0, r = chunks[c]
        norm_into(lambda o, g: hb[o, g, r0:r0 + r, :], gm_ref, r0, r)

    for c in range(last):
        forward(c)
    relay(last)
    for c in range(last):
        for way in range(2):
            chunk_link(3, c, way).wait_recv()
        norm_chunk(c)
    reduce(last)
    for way in range(2):
        chunk_link(2, last, way).wait_recv()
    chunk_link(3, last, 0).wait_recv()
    norm_chunk(last)
    for c in range(len(chunks)):
        for way in range(2):
            for kind in range(3):
                chunk_link(kind, c, way).wait_send()
        for way in range(2 if c < last else 1):
            chunk_link(3, c, way).wait_send()

    def up(j, _):
        for which in range(2):
            up_copy(j, which).wait()
        gate, value = products(
            lambda k, m: norm[:, k:k + m], [lambda k, m, at=region(2 * j + which): arena[rows(at + k, m), :] for which in range(2)], d, BN)
        hid[:, columns(j)] = (jax.nn.silu(gate) * value).astype(BF16)

        @pl.when(j + half < n_up)
        def _():
            up_copy(j + half, 0).start()
            up_copy(j + half, 1).start()

        for e in range(half):
            @pl.when(j == n_up - half + e)
            def _():
                for v in (2 * e, 2 * e + 1):
                    down_copy(v).start()
        return 0
    lax.fori_loop(0, n_up, up, 0)

    def down(p):
        two = (2 * p, 2 * p + 1)
        for v in two:
            down_copy(v).wait()
        found = products(
            lambda k, m: hid[:, k:k + m], [lambda k, m, at=region(2 * n_up + v): arena[rows(at + k, m), :] for v in two], ff, BN)
        for v in two:
            if v + 2 * half < len(blocks):
                down_copy(v + 2 * half).start()
        return found

    def group_link(kind, g, way, owner=None):
        straight = kind == 3 and g >= groups - 2
        lanes = half_lanes[way] if kind == 3 and not straight else slice(0, BN)
        owner = me if owner is None else owner
        if kind < 2:
            src, dst = ((far_terms, far_got), (terms, got))[kind]
            return link(4 + kind, g, way, src.at[way, g], dst.at[way, g])
        states = yb.at[owner, g, :, lanes]
        return link(4 + kind, g, way, states, states, FAR if straight else None)

    def send_far(t, group):
        for way in range(2):
            far_terms[way, group] = t[:, half_lanes[way]].astype(BF16)
        for way in range(2):
            group_link(0, group, way).start()

    def send_side(t, g, way):
        group_link(0, g, way).wait_recv()
        for lanes in range(2):
            u = t[:, half_lanes[lanes]]
            if lanes == way:
                u = u + far_got[way, g].astype(F32)
            terms[way, g, :, half_lanes[lanes]] = u.astype(BF16)
        group_link(1, g, way).start()

    def finish(g):
        for way in range(2):
            group_link(1, g, way).wait_recv()
        s = own[g]
        for way in range(2):
            s += got[way, g].astype(F32)
        yb[me, g] = (hb[me, g].astype(F32) + s).astype(BF16)
        for way in range(2):
            group_link(2, g, way).start()
        if g >= groups - 2:
            group_link(3, g, 0).start()

    def pass_on(g):
        for way in range(2):
            source = device(to[1 - way])
            group_link(2, g, way, source).wait_recv()
            group_link(3, g, way, source).start()

    sent, done = {}, {}
    for p, two in enumerate(order):
        for (rel, g), t in zip(two, down(p)):
            if rel == FAR:
                send_far(t, g)
            elif rel == OWN:
                own[g] = t
            else:
                send_side(t, g, to.index(rel))
                sent[g] = p
        mine = {g for two_ in order[:p + 1] for rel, g in two_ if rel == OWN}
        for g in range(groups):
            if g in done and done[g] is not None and g < groups - 2 and p >= done[g] + 2:
                pass_on(g)
                done[g] = None
        for g in range(groups):
            if g not in done and g in mine and g in sent and p >= sent[g] + 2:
                finish(g)
                done[g] = p
    for g in range(groups):
        if g not in done:
            finish(g)
            done[g] = len(order)
    for g in range(groups - 2):
        if done[g] is not None:
            pass_on(g)

    for g in range(groups):
        straight = g >= groups - 2
        for way in range(2):
            for kind in range(3):
                group_link(kind, g, way).wait_send()
            if straight:
                group_link(2, g, way).wait_recv()
        for way in range(1 if straight else 2):
            group_link(3, g, way).wait_send()
            group_link(3, g, way).wait_recv()
        for o in range(n):
            y_ref[:, rows(o * own_cols + g * BN, BN, BN)] = yb[o, g]


def solution(mesh):
    n = mesh.shape["tp"]

    def step(x, k_cache, v_cache, gain_a, wq, wo, gain_m, w_gate, w_up, w_down):
        batch, d = x.shape
        cache, kv_heads = k_cache.shape[1:3]
        keys = cache * kv_heads
        heads = wq.shape[1] // HEAD
        ff = w_gate.shape[1]
        half, groups = 7, d // n // BN
        kv_slots = half * d // (2 * keys)
        pairs = batch // 2
        after = []
        for t in range(half):
            r = (t + 3) % half
            need = [s for s in range(kv_slots) if s * 2 * keys < (r + 1) * d and (s + 1) * 2 * keys > r * d]
            after.append(max(p for p in range(pairs - kv_slots, pairs) if p % kv_slots in need))
        chunks = ((0, batch * 3 // 4), (batch * 3 // 4, batch // 4))
        cfg = dict(n=n, batch=batch, d=d, keys=keys, heads=heads, ff=ff, chunks=chunks, relay_after=batch // 16, reduce_after=batch * 3 // 16, after=after)

        i = np.arange(HEAD // 2)
        angle = (cache - 1) * THETA ** (-i / (HEAD // 2))
        cos, sin = np.cos(angle), np.sin(angle)
        turn = jnp.asarray(np.stack([np.concatenate([cos, cos]), np.concatenate([-sin, sin])]), F32)

        any_, vmem = pl.BlockSpec(memory_space=pl.ANY), pl.BlockSpec(memory_space=pltpu.VMEM)
        dma = pltpu.SemaphoreType.DMA
        nc = len(chunks)
        return pl.pallas_call(
            functools.partial(kernel, cfg),
            out_shape=jax.ShapeDtypeStruct(x.shape, x.dtype),
            in_specs=[any_, any_, any_, vmem, any_, any_, vmem, any_, any_, any_, vmem],
            out_specs=vmem,
            scratch_shapes=[
                pltpu.VMEM((2 * half * d, BN), BF16),
                pltpu.VMEM((batch, d), BF16),
                pltpu.VMEM((batch, d), BF16),
                pltpu.VMEM((heads, batch, HEAD), F32),
                pltpu.VMEM((batch * PAD, HEAD), F32),
                pltpu.VMEM((batch * PAD, HEAD), F32),
                pltpu.VMEM((batch, heads * HEAD), BF16),
                pltpu.VMEM((2, groups, batch, BN // 2), BF16),
                pltpu.VMEM((2, groups, batch, BN // 2), BF16),
                pltpu.VMEM((2, groups, batch, BN), F32),
                pltpu.VMEM((2, groups, batch, BN), BF16),
                pltpu.VMEM((2, groups, batch, BN), BF16),
                pltpu.VMEM((groups, batch, BN), F32),
                pltpu.VMEM((n, groups, batch, BN), BF16),
                pltpu.VMEM((batch, ff), BF16),
                pltpu.VMEM((n, groups, batch, BN), BF16),
                pltpu.VMEM((2 * PAD, keys), F32),
                pltpu.VMEM((2 * PAD, keys), F32),
                dma((half + d // BN,)), dma((kv_slots, 4)), dma((1,)),
                *[dma((2, nc))] * 8, *[dma((2, groups))] * 8,
            ],
            compiler_params=pltpu.CompilerParams(collective_id=0, has_side_effects=True, vmem_limit_bytes=67043328),
        )(x, k_cache.reshape(batch, keys, HEAD), v_cache.reshape(batch, keys, HEAD), gain_a.reshape(1, d), wq, wo,
          gain_m.reshape(1, d), w_gate, w_up, w_down, turn)

    states, cache, columns_, rows_of = P("dp", None), P("dp", None, "tp", None), P(None, "tp"), P("tp", None)
    return jax.shard_map(
        step,
        mesh=mesh,
        in_specs=(states, cache, cache, P(None), columns_, rows_of, P(None), columns_, columns_, rows_of),
        out_specs=states,
        check_vma=False,
    )
```

time: 184 us -> 151 us (0.82)
  Pallas kernels: 178 us -> 146 us
    pallas_call x1, Pallas kernels: 178 us -> 146 us  [step(): pl.pallas_call(functools.partial(kernel, cfg), out_shape=jax.ShapeDtypeSt...]
where the time goes in v2:
time: 151 us; the launch traced here: 150 us
  Pallas kernels  146 us (97%)
  local copies, waits for them, and re-layouts  4.82 us (3%)
    pallas_call x1, Pallas kernels, step(): pl.pallas_call(functools.partial(kernel, cfg), out_shape=jax.ShapeDtypeSt...  146 us

profile of v2, /device:TPU:112, one launch (start us, length us, event | category | flops | bytes accessed | tf_op | source)
XLA Modules:
  0.0 150.4 jit_solution(11021954878390571179)
XLA Ops:
  0.0 1.3 reshape.14.ga_ref
  1.3 1.3 reshape.15.gm_ref
  2.7 145.6 %shard_map.109 = bf16[64,7168]{1,0:T(8,128)(2,1)} custom-call(bf16[64,7168]{1,0:T(8,128)(2,1)} %x_hbm.1, bf16[64,4096,128]{2,1,0:T(8,128)(2,1)} %bitcast.k_hbm, bf16[64,4096,128]{2,1,0:T(8,128)(2,1)} %bitcast.1.v_hbm, bf16[1,7168]{1,0:T(2,128)(2,1)} %reshape.14.ga_ref, bf16[7168,1792]{1,0:T(8,128)(2,1)} %wq_hbm.1, bf16[1792,7168]{1,0:T(8,128)(2,1)} %wo_hbm.1, ...), custom_call_target="tpu_custom_call" | custom-call | tf_op jit(solution)/shard_map/pallas_call | solution.py:513
  148.3 2.2 %copy.13 = bf16[64,7168]{1,0:T(8,128)(2,1)} copy(bf16[64,7168]{1,0:T(8,128)(2,1)} %shard_map.109) | data formatting | bytes 1835008

commit v3 on v2

--- a/solution.py
+++ b/solution.py
@@ -38,7 +38,7 @@
 
 
 def kernel(cfg, x_hbm, k_hbm, v_hbm, ga_ref, wq_hbm, wo_hbm, gm_ref, wg_hbm, wu_hbm, wd_hbm, turn_ref, y_ref,
-           arena, x_ref, norm, qt, qs, os_, seen, far_terms, far_got, side, terms, got, own, hb, hid, yb, sc_a, sc_b,
+           arena, x_ref, norm, gain_a, gain_m, qt, qs, os_, seen, far_terms, far_got, side, terms, got, own, hb, hid, yb, sc_a, sc_b,
            blk_sem, kv_sem, x_sem, *link_sems):
     n, batch, d, keys, heads, ff, chunks = cfg["n"], cfg["batch"], cfg["d"], cfg["keys"], cfg["heads"], cfg["ff"], cfg["chunks"]
     qw = heads * HEAD
@@ -130,12 +130,16 @@
         def put(o, _):
             for g in range(groups):
                 at = columns(o * groups + g)
-                norm[r0:r0 + r, at] = (read(o, g).astype(F32) * s * gain_ref[:, at].astype(F32)).astype(BF16)
+                row = (o * groups + g) * (BN // HEAD)
+                gain = jnp.concatenate([gain_ref[pl.ds(row + k, 1), :] for k in range(BN // HEAD)], 1)
+                norm[r0:r0 + r, at] = (read(o, g).astype(F32) * s * gain).astype(BF16)
             return 0
         lax.fori_loop(0, n, put, 0)
 
+    gain_a[...] = ga_ref[...].astype(F32)
+    gain_m[...] = gm_ref[...].astype(F32)
     x_copy.wait()
-    norm_into(lambda o, g: x_ref[:, columns(o * groups + g)], ga_ref, 0, batch)
+    norm_into(lambda o, g: x_ref[:, columns(o * groups + g)], gain_a, 0, batch)
     qs[...] = jnp.zeros_like(qs)
 
     def with_norm(at):
@@ -346,7 +350,7 @@
         up_copy(t // 2, t % 2).start()
     def norm_chunk(c):
         r0, r = chunks[c]
-        norm_into(lambda o, g: hb[o, g, r0:r0 + r, :], gm_ref, r0, r)
+        norm_into(lambda o, g: hb[o, g, r0:r0 + r, :], gain_m, r0, r)
 
     for c in range(last):
         forward(c)
@@ -519,6 +523,8 @@
                 pltpu.VMEM((2 * half * d, BN), BF16),
                 pltpu.VMEM((batch, d), BF16),
                 pltpu.VMEM((batch, d), BF16),
+                pltpu.VMEM((d // HEAD, HEAD), F32),
+                pltpu.VMEM((d // HEAD, HEAD), F32),
                 pltpu.VMEM((heads, batch, HEAD), F32),
                 pltpu.VMEM((batch * PAD, HEAD), F32),
                 pltpu.VMEM((batch * PAD, HEAD), F32),
@@ -538,8 +544,8 @@
                 *[dma((2, nc))] * 8, *[dma((2, groups))] * 8,
             ],
             compiler_params=pltpu.CompilerParams(collective_id=0, has_side_effects=True, vmem_limit_bytes=67043328),
-        )(x, k_cache.reshape(batch, keys, HEAD), v_cache.reshape(batch, keys, HEAD), gain_a.reshape(1, d), wq, wo,
-          gain_m.reshape(1, d), w_gate, w_up, w_down, turn)
+        )(x, k_cache.reshape(batch, keys, HEAD), v_cache.reshape(batch, keys, HEAD), gain_a.reshape(d // HEAD, HEAD), wq, wo,
+          gain_m.reshape(d // HEAD, HEAD), w_gate, w_up, w_down, turn)
 
     states, cache, columns_, rows_of = P("dp", None), P("dp", None, "tp", None), P(None, "tp"), P("tp", None)
     return jax.shard_map(

time: 151 us -> 148 us (0.980)
  local copies, waits for them, and re-layouts: 4.82 us -> 2.16 us
    reshape x2 -> x0, local copies, waits for them, and re-layouts: 2.66 us -> none  [the longest x1 1.34 us: step(): gain_a.reshape(1, d)]
where the time goes in v3:
time: 148 us
  Pallas kernels  146 us (99%)
  local copies, waits for them, and re-layouts  2.16 us (1%)
    pallas_call x1, Pallas kernels, step(): pl.pallas_call(functools.partial(kernel, cfg), out_shape=jax.ShapeDtypeSt...  146 us

profile of v3, /device:TPU:112, one launch (start us, length us, event | category | flops | bytes accessed | tf_op | source)
XLA Modules:
  0.0 147.7 jit_solution(12922906260725972826)
XLA Ops:
  0.0 145.5 %shard_map.109 = bf16[64,7168]{1,0:T(8,128)(2,1)} custom-call(bf16[64,7168]{1,0:T(8,128)(2,1)} %x_hbm.1, bf16[64,4096,128]{2,1,0:T(8,128)(2,1)} %bitcast.k_hbm, bf16[64,4096,128]{2,1,0:T(8,128)(2,1)} %bitcast.1.v_hbm, bf16[56,128]{1,0:T(8,128)(2,1)} %bitcast.4, bf16[7168,1792]{1,0:T(8,128)(2,1)} %wq_hbm.1, bf16[1792,7168]{1,0:T(8,128)(2,1)} %wo_hbm.1, ...), custom_call_target="tpu_custom_call" | custom-call | tf_op jit(solution)/shard_map/pallas_call | solution.py:517
  145.6 2.2 %copy.13 = bf16[64,7168]{1,0:T(8,128)(2,1)} copy(bf16[64,7168]{1,0:T(8,128)(2,1)} %shard_map.109) | data formatting | bytes 1835008
